TPU v7x, 32 devices: a whole 2x2x4 slice. The times are simulated.
32 devices in a mesh: dp: 16 (over z, y, core), tensor: 2 (over x).
Axes of the slice: x: 2, y: 2, z: 4, core: 2. Of those that a mesh axis runs over, the one named last changes fastest.
Arguments:
- layer_input: bfloat16 [16384, 1024], P(('dp', 'tensor')), may hold values from -6 to 6
- segments: int32 [16384], P('dp'), may hold values from 0 to 127, never falling along the last dimension, each value on 1 to 256 neighbouring positions
- w_qkv: bfloat16 [1024, 3, 1024], P(None, None, 'tensor'), may hold values from -0.1875 to 0.1875
- w_out: bfloat16 [1024, 1024], P('tensor'), may hold values from -2 to 2
- w_up: bfloat16 [1024, 4096], P(None, 'tensor'), may hold values from -0.1875 to 0.1875
- w_down: bfloat16 [4096, 1024], P('tensor'), may hold values from -0.09375 to 0.09375
- norm1_gain: float32 [1024], replicated, may hold values from 0.5 to 1.5
- norm1_bias: float32 [1024], replicated, may hold values from -3 to 3
- norm2_gain: float32 [1024], replicated, may hold values from 0.5 to 1.5
- norm2_bias: float32 [1024], replicated, may hold values from -3 to 3
- out_grad: bfloat16 [16384, 1024], P(('dp', 'tensor')), may hold values from -6 to 6
Outputs:
- output: bfloat16 [16384, 1024], P(('dp', 'tensor'))
- input_grad: bfloat16 [16384, 1024], P(('dp', 'tensor'))
- grad_qkv: float32 [1024, 3, 1024], P(None, None, 'tensor')
- grad_out: float32 [1024, 1024], P('tensor')
- grad_up: float32 [1024, 4096], P(None, 'tensor')
- grad_down: float32 [4096, 1024], P('tensor')
- grad_gain1: float32 [1024], replicated
- grad_bias1: float32 [1024], replicated
- grad_gain2: float32 [1024], replicated
- grad_bias2: float32 [1024], replicated
Inputs may be any that keep to these rules, and one draw needn't show every extreme that they name: `segments`: segment ids never fall along the tokens; each protein has 1 to 256 tokens and attends only within its packed row of 512.
All inputs are finite; a program needn't handle non-finite values.
Results may differ from a plain program's by a relative error of at most 0.02.
Values may be sent and summed in bfloat16 or wider, within the bound.
A program may use at most 192 MiB of HBM per device.

v0:
```python
import jax
import jax.numpy as jnp
from jax import lax
from jax.sharding import PartitionSpec as P

HEAD_DIM = 64
ROW_LEN = 512
EPS = 1e-12
NEG_LARGE = -1e30
SQRT_HALF = 0.7071067811865476
INV_ROOT_TWO_PI = 0.3989422804014327


def gelu_exact(values):
    return 0.5 * values * (1.0 + lax.erf(values * SQRT_HALF))


def gelu_slope(values):
    return (
        0.5 * (1.0 + lax.erf(values * SQRT_HALF))
        + values * jnp.exp(-0.5 * values * values) * INV_ROOT_TWO_PI
    )


def layer_norm(values, gain, bias):
    average = jnp.mean(values, axis=-1, keepdims=True)
    centred = values - average
    inverse = lax.rsqrt(jnp.mean(centred * centred, axis=-1, keepdims=True) + EPS)
    normed = centred * inverse
    return (normed * gain + bias, normed, inverse)


def norm_back(grad, normed, inverse, gain):
    scaled = grad * gain
    return inverse * (
        scaled
        - jnp.mean(scaled, axis=-1, keepdims=True)
        - normed * jnp.mean(scaled * normed, axis=-1, keepdims=True)
    )


def masked_scores(queries, keys, row_segments, factor):
    scores = jnp.einsum("qhd,khd->hqk", queries, keys, preferred_element_type=jnp.float32) * factor
    same = row_segments[:, None] == row_segments[None, :]
    return jnp.where(same[None], scores, NEG_LARGE)


def contract_rows(left, right):
    return lax.dot_general(
        left, right, (((0,), (0,)), ((), ())), preferred_element_type=jnp.float32
    )


def contract_cols(left, right):
    return lax.dot_general(
        left, right, (((1,), (1,)), ((), ())), preferred_element_type=jnp.float32
    )


def body(
    layer_input,
    segments,
    w_qkv,
    w_out,
    w_up,
    w_down,
    norm1_gain,
    norm1_bias,
    norm2_gain,
    norm2_bias,
    out_grad,
):
    head_width = HEAD_DIM
    row_length = ROW_LEN
    factor = head_width ** (-0.5)
    qkv_use, out_use = (w_qkv, w_out)
    source = lax.all_gather(layer_input, "tensor", axis=0, tiled=True)
    local_width = qkv_use.shape[2]
    local_heads = local_width // head_width
    group_rows = source.shape[0]
    blocks = group_rows // row_length
    joined = jnp.einsum("td,dsc->tsc", source, qkv_use, preferred_element_type=jnp.float32).astype(
        jnp.bfloat16
    )
    joined_blocks = joined.reshape(blocks, row_length, 3, local_heads, head_width)
    segment_blocks = segments.reshape(blocks, row_length)

    def attend(pack):
        block, row_segments = pack
        scores = masked_scores(block[:, 0], block[:, 1], row_segments, factor)
        top = jnp.max(scores, axis=-1, keepdims=True)
        expo = jnp.exp(scores - top)
        total = jnp.sum(expo, axis=-1, keepdims=True)
        probs = (expo / total).astype(jnp.bfloat16)
        mixed = jnp.einsum("hqk,khd->qhd", probs, block[:, 2], preferred_element_type=jnp.float32)
        return (
            mixed.reshape(row_length, local_width).astype(jnp.bfloat16),
            (top + jnp.log(total))[..., 0],
        )

    attended, log_totals = lax.map(attend, (joined_blocks, segment_blocks))
    attended = attended.reshape(group_rows, local_width)
    attn_out = lax.psum_scatter(
        jnp.dot(attended, out_use, preferred_element_type=jnp.float32).astype(jnp.bfloat16),
        "tensor",
        scatter_dimension=0,
        tiled=True,
    ).astype(jnp.float32)
    hidden, normed_one, inverse_one = layer_norm(
        layer_input.astype(jnp.float32) + attn_out, norm1_gain, norm1_bias
    )
    hidden_low = hidden.astype(jnp.bfloat16)
    hidden_group = lax.all_gather(hidden_low, "tensor", axis=0, tiled=True)
    upper = jnp.dot(hidden_group, w_up, preferred_element_type=jnp.float32)
    active = gelu_exact(upper).astype(jnp.bfloat16)
    ffn_out = lax.psum_scatter(
        jnp.dot(active, w_down, preferred_element_type=jnp.float32).astype(jnp.bfloat16),
        "tensor",
        scatter_dimension=0,
        tiled=True,
    ).astype(jnp.float32)
    result, normed_two, inverse_two = layer_norm(hidden + ffn_out, norm2_gain, norm2_bias)
    grad_result = out_grad.astype(jnp.float32)
    grad_gain2 = jnp.sum(grad_result * normed_two, axis=0)
    grad_bias2 = jnp.sum(grad_result, axis=0)
    grad_second = norm_back(grad_result, normed_two, inverse_two, norm2_gain)
    branch_low = grad_second.astype(jnp.bfloat16)
    branch_group = lax.all_gather(branch_low, "tensor", axis=0, tiled=True)
    grad_active = contract_cols(branch_group, w_down)
    grad_upper = (grad_active * gelu_slope(upper)).astype(jnp.bfloat16)
    grad_down = contract_rows(active, branch_group)
    grad_up = contract_rows(hidden_group, grad_upper)
    hidden_part = lax.psum_scatter(
        contract_cols(grad_upper, w_up).astype(jnp.bfloat16),
        "tensor",
        scatter_dimension=0,
        tiled=True,
    ).astype(jnp.float32)
    grad_hidden = grad_second + hidden_part
    grad_gain1 = jnp.sum(grad_hidden * normed_one, axis=0)
    grad_bias1 = jnp.sum(grad_hidden, axis=0)
    grad_first = norm_back(grad_hidden, normed_one, inverse_one, norm1_gain)
    attn_low = grad_first.astype(jnp.bfloat16)
    attn_group = lax.all_gather(attn_low, "tensor", axis=0, tiled=True)
    grad_mixed = contract_cols(attn_group, out_use).astype(jnp.bfloat16)
    grad_out_w = contract_rows(attended, attn_group)
    grad_mixed_blocks = grad_mixed.reshape(blocks, row_length, local_heads, head_width)

    def attend_back(pack):
        block, row_segments, log_total, grad_block = pack
        queries = block[:, 0]
        keys = block[:, 1]
        values = block[:, 2]
        scores = masked_scores(queries, keys, row_segments, factor)
        probs = jnp.exp(scores - log_total[..., None])
        grad_probs = jnp.einsum(
            "qhd,khd->hqk", grad_block, values, preferred_element_type=jnp.float32
        )
        grad_scores = probs * (grad_probs - jnp.sum(probs * grad_probs, axis=-1, keepdims=True))
        grad_scores = grad_scores.astype(jnp.bfloat16)
        grad_query = (
            jnp.einsum("hqk,khd->qhd", grad_scores, keys, preferred_element_type=jnp.float32)
            * factor
        )
        grad_key = (
            jnp.einsum("hqk,qhd->khd", grad_scores, queries, preferred_element_type=jnp.float32)
            * factor
        )
        grad_value = jnp.einsum(
            "hqk,qhd->khd",
            probs.astype(jnp.bfloat16),
            grad_block,
            preferred_element_type=jnp.float32,
        )
        stacked = jnp.stack([grad_query, grad_key, grad_value], axis=1)
        return stacked.reshape(row_length, 3, local_width).astype(jnp.bfloat16)

    grad_joined = lax.map(
        attend_back, (joined_blocks, segment_blocks, log_totals, grad_mixed_blocks)
    )
    grad_joined = grad_joined.reshape(group_rows, 3, local_width)
    grad_qkv_w = jnp.einsum("td,tsc->dsc", source, grad_joined, preferred_element_type=jnp.float32)
    input_part = lax.psum_scatter(
        jnp.einsum("tsc,dsc->td", grad_joined, qkv_use, preferred_element_type=jnp.float32).astype(
            jnp.bfloat16
        ),
        "tensor",
        scatter_dimension=0,
        tiled=True,
    ).astype(jnp.float32)
    grad_input = grad_first + input_part
    summed_qkv, summed_out, summed_up, summed_down = (
        lax.psum(grad_qkv_w.astype(jnp.bfloat16), "dp").astype(jnp.float32),
        lax.psum(grad_out_w.astype(jnp.bfloat16), "dp").astype(jnp.float32),
        lax.psum(grad_up.astype(jnp.bfloat16), "dp").astype(jnp.float32),
        lax.psum(grad_down.astype(jnp.bfloat16), "dp").astype(jnp.float32),
    )
    summed_gain1, summed_bias1, summed_gain2, summed_bias2 = lax.psum(
        (grad_gain1, grad_bias1, grad_gain2, grad_bias2), ("dp", "tensor")
    )
    return (
        result.astype(jnp.bfloat16),
        grad_input.astype(jnp.bfloat16),
        summed_qkv,
        summed_out,
        summed_up,
        summed_down,
        summed_gain1,
        summed_bias1,
        summed_gain2,
        summed_bias2,
    )


def solution(mesh):
    return jax.shard_map(
        body,
        mesh=mesh,
        in_specs=(
            P(("dp", "tensor"), None),
            P("dp"),
            P(None, None, "tensor"),
            P("tensor", None),
            P(None, "tensor"),
            P("tensor", None),
            P(),
            P(),
            P(),
            P(),
            P(("dp", "tensor"), None),
        ),
        out_specs=(
            P(("dp", "tensor"), None),
            P(("dp", "tensor"), None),
            P(None, None, "tensor"),
            P("tensor", None),
            P(None, "tensor"),
            P("tensor", None),
            P(),
            P(),
            P(),
            P(),
        ),
        check_vma=False,
    )
```

profile of v0, /device:TPU:0, one launch (start us, length us, event | category | flops | bytes accessed | tf_op | source)
XLA Modules:
  0.0 702.6 jit_solution(4263438143487047636)
XLA Ops:
  8.8 36.6 %all-gather.5.cloned.1.call-done = bf16[1024,1024]{1,0:T(8,128)(2,1)} async-done(((bf16[512,1024]{1,0:T(8,128)(2,1)}), bf16[1024,1024]{1,0:T(8,128)(2,1)}) %all-gather.5.cloned.1.call-update) | async-done | bytes 2097168 | tf_op jit(solution)/shard_map/all_gather | solution.py:77
  45.4 6.3 convolution_convert_fusion.2
  51.7 8.9 %reshape.242 = bf16[2,512,3,8,64]{4,3,1,0,2:T(8,128)(2,1)} reshape(bf16[1024,3,512]{2,0,1:T(8,128)(2,1)} %convolution_convert_fusion.2) | data formatting | bytes 6291456 | tf_op jit(solution)/shard_map/reshape | solution.py:85
  60.6 7.6 %copy.35 = bf16[2,512,3,8,64]{1,4,3,2,0:T(8,128)(2,1)} copy(bf16[2,512,3,8,64]{4,3,1,0,2:T(8,128)(2,1)} %reshape.242) | data formatting | bytes 6291456 | tf_op jit(solution)/shard_map/while | solution.py:101
  68.2 24.3 %while.22 = (s32[]{:T(128)}, bf16[2,512,512]{2,1,0:T(8,128)(2,1)}, f32[2,8,512]{2,1,0:T(8,128)S(1)}, bf16[2,512,3,8,64]{1,4,3,2,0:T(8,128)(2,1)}, s32[2,512]{1,0:T(2,128)S(1)}, /*index=5*/s32[]{:T(128)}) while((s32[]{:T(128)}, bf16[2,512,512]{2,1,0:T(8,128)(2,1)}, f32[2,8,512]{2,1,0:T(8,128)S(1)}, bf16[2,512,3,8,64]{1,4,3,2,0:T(8,128)(2,1)}, ...), condition=%wide.region_3.4_spmd, body=%wide.region_0.3_spmd.sunk | while | flops 562556928 | bytes 33692240 | solution.py:101
  73.2 3.2 fusion.87
  85.4 3.2 fusion.87
  92.5 4.1 convolution_convert_fusion.5
  96.7 32.0 %reduce-scatter.5.cloned.1.call-done = bf16[512,1024]{1,0:T(8,128)(2,1)} async-done(((bf16[1024,1024]{1,0:T(8,128)(2,1)}), bf16[512,1024]{1,0:T(8,128)(2,1)}) %reduce-scatter.5.cloned.1.call-update) | async-done | bytes 1048592 | tf_op jit(solution)/shard_map/reduce_scatter | solution.py:103
  134.6 33.0 %all-gather.7.cloned.1.call-done = bf16[1024,1024]{1,0:T(8,128)(2,1)} async-done(((bf16[512,1024]{1,0:T(8,128)(2,1)}), bf16[1024,1024]{1,0:T(8,128)(2,1)}) %all-gather.7.cloned.1.call-update) | async-done | bytes 2097168 | tf_op jit(solution)/shard_map/all_gather | solution.py:113
  167.6 9.5 %multiply_convert_fusion.1 = (bf16[1024,2048]{1,0:T(8,128)(2,1)S(1)}, f32[1024,2048]{1,0:T(8,128)}) fusion(bf16[1024,1024]{1,0:T(8,128)(2,1)} %all-gather.7.cloned.1.call-done, bf16[1024,2048]{1,0:T(8,128)(2,1)} %param.19), kind=kOutput, calls=%fused_computation.55 | convolution fusion | flops 4305453056 | bytes 18874368 | tf_op jit(solution)/shard_map/dot_general | solution.py:114
  179.1 5.6 convolution_convert_fusion.4
  184.8 32.0 %reduce-scatter.7.cloned.1.call-done = bf16[512,1024]{1,0:T(8,128)(2,1)} async-done(((bf16[1024,1024]{1,0:T(8,128)(2,1)}), bf16[512,1024]{1,0:T(8,128)(2,1)}) %reduce-scatter.7.cloned.1.call-update) | async-done | bytes 1048592 | tf_op jit(solution)/shard_map/reduce_scatter | solution.py:116
  216.8 2.8 fusion.49
  221.6 2.9 fusion.47
  224.7 33.0 %all-gather.9.cloned.1.call-done = bf16[1024,1024]{1,0:T(8,128)(2,1)} async-done(((bf16[512,1024]{1,0:T(8,128)(2,1)}), bf16[1024,1024]{1,0:T(8,128)(2,1)}) %all-gather.9.cloned.1.call-update) | async-done | bytes 2097168 | tf_op jit(solution)/shard_map/all_gather | solution.py:128
  257.7 10.3 %fusion.31 = bf16[1024,2048]{1,0:T(8,128)(2,1)S(1)} fusion(f32[1024,2048]{1,0:T(8,128)} %get-tuple-element.165, bf16[1024,1024]{1,0:T(8,128)(2,1)} %all-gather.9.cloned.1.call-done, bf16[2048,1024]{1,0:T(8,128)(2,1)} %param.20), kind=kOutput, calls=%fused_computation.54 | convolution fusion | flops 4315938816 | bytes 18874368 | tf_op jit(solution)/shard_map/dot_general | solution.py:55
  270.0 5.7 convolution_convert_fusion.3
  275.8 32.0 %reduce-scatter.9.cloned.1.call-done = bf16[512,1024]{1,0:T(8,128)(2,1)} async-done(((bf16[1024,1024]{1,0:T(8,128)(2,1)}), bf16[512,1024]{1,0:T(8,128)(2,1)}) %reduce-scatter.9.cloned.1.call-update) | async-done | bytes 1048592 | tf_op jit(solution)/shard_map/reduce_scatter | solution.py:133
  307.8 4.4 multiply_reduce_fusion.1
  312.3 2.5 fusion.46
  314.9 33.2 %all-gather.11.cloned.1.call-done = bf16[1024,1024]{1,0:T(8,128)(2,1)} async-done(((bf16[512,1024]{1,0:T(8,128)(2,1)}), bf16[1024,1024]{1,0:T(8,128)(2,1)}) %all-gather.11.cloned.1.call-update) | async-done | bytes 2097168 | tf_op jit(solution)/shard_map/all_gather | solution.py:144
  348.1 4.1 convolution_convert_fusion.7
  352.2 4.3 reshape.241
  356.5 3.3 copy.39
  359.8 39.5 %while.23 = (s32[]{:T(128)}, bf16[2,512,3,512]{3,1,0,2:T(8,128)(2,1)}, bf16[2,512,3,8,64]{1,4,3,2,0:T(8,128)(2,1)}, s32[2,512]{1,0:T(2,128)S(1)}, f32[2,8,512]{2...) while((s32[]{:T(128)}, bf16[2,512,3,512]{3,1,0,2:T(8,128)(2,1)}, ...), condition=%wide.region_17.18_spmd, body=%wide.region_15.17_spmd.sunk | while | flops 1376776192 | bytes 86104704 | solution.py:178
  362.9 2.9 multiply_reduce_fusion.7
  365.8 2.7 multiply_convert_fusion.3
  370.7 2.3 fusion.93
  374.3 2.6 copy.59
  376.9 2.7 constant_dynamic-update-slice_fusion.5
  382.7 2.9 multiply_reduce_fusion.7
  385.6 2.7 multiply_convert_fusion.3
  390.4 2.3 fusion.93
  394.0 2.6 copy.59
  396.6 2.7 constant_dynamic-update-slice_fusion.5
  399.3 6.6 bitcast_convert_fusion
  406.1 9.6 %convolution_convert_fusion = bf16[2048,1024]{1,0:T(8,128)(2,1)} fusion(bf16[1024,2048]{1,0:T(8,128)(2,1)} %copy-done.27, bf16[1024,1024]{1,0:T(8,128)(2,1)} %all-gather.9.cloned.1.call-done), kind=kOutput, calls=%fused_computation.58 | convolution fusion | flops 4297064448 | bytes 10485760 | tf_op jit(solution)/shard_map/dot_general | solution.py:49
  415.7 6.2 convolution_convert_fusion.1
  422.0 2.3 convolution_convert_fusion.6
  424.3 4.9 convert_bitcast_fusion
  429.9 40.7 %all-reduce = (f32[1024]{0:T(1024)}, f32[1024]{0:T(1024)}, f32[1024]{0:T(1024)}, f32[1024]{0:T(1024)}) all-reduce(f32[1024]{0:T(1024)S(1)} %copy-done.17, f32[1024]{0:T(1024)S(1)} %copy-done.18, f32[1024]{0:T(1024)S(1)} %copy-done.14, f32[1024]{0:T(1024)S(1)} %copy-done.15), channel_id=1, replica_groups=mesh['dp'=16,'tensor'=2] {'dp','tensor'}, use_global_device_ids=true, to_apply=%region_24.25 | all-reduce | flops 4096 | bytes 32768 | tf_op jit(solution)/shard_map/psum | solution.py:198
  470.5 3.2 add_convert_fusion
  473.7 202.7 %all-reduce.4.cloned.1.call-done = (bf16[1024,3,512]{0,2,1:T(8,128)(2,1)}, bf16[512,1024]{1,0:T(8,128)(2,1)}, bf16[1024,2048]{1,0:T(8,128)(2,1)}, bf16[2048,1024]{1,0:T(8,128)(2,1)}) async-done(((bf16[1024,3,512]{0,2,1:T(8,128)(2,1)}, bf16[512,1024]{1,0:T(8,128)(2,1)}, bf16[1024,2048]{1,0:T(8,128)(2,1)}, bf16[2048,1024]{1,0:T(8,128)(2,1)}), (bf16[1024,3,512]{0,2,1:T(8,128)(2,1)}, ...) | async-done | bytes 12582928 | tf_op jit(solution)/shard_map/psum | solution.py:193
  676.4 6.8 convert_element_type.142
  683.2 4.4 convert_element_type.144
  687.7 5.4 copy.42
  693.1 2.8 convert_element_type.140
  (125 shorter events, 45.8 us)
Async XLA Ops:
  7.2 38.2 %copy-start = (bf16[1024,3,512]{2,0,1:T(8,128)(2,1)S(1)}, bf16[1024,3,512]{2,0,1:T(8,128)(2,1)}, u32[]{:S(2)}) copy-start(bf16[1024,3,512]{2,0,1:T(8,128)(2,1)} %param.17) | copy-start | bytes 9437188
  7.2 38.2 %all-gather.5.cloned.1.call-start = ((), (), s32[]{:S(2)}) async-start(), calls=%async_computation.4 | async-start | bytes 3145728 | tf_op jit(solution)/shard_map/all_gather | solution.py:77
  7.9 120.8 %reduce-scatter.5.cloned.1.call-start = ((), (), s32[]{:S(2)}) async-start(), calls=%async_computation.5 | async-start | bytes 3145728 | tf_op jit(solution)/shard_map/reduce_scatter | solution.py:103
  96.6 36.2 %copy-start.12 = (f32[1024]{0:T(1024)S(1)}, f32[1024]{0:T(1024)}, u32[]{:S(2)}) copy-start(f32[1024]{0:T(1024)} %param.21) | copy-start | bytes 12292
  96.6 36.2 %copy-start.16 = (f32[1024]{0:T(1024)S(1)}, f32[1024]{0:T(1024)}, u32[]{:S(2)}) copy-start(f32[1024]{0:T(1024)} %param.22) | copy-start | bytes 12292
  96.6 71.0 %all-gather.7.cloned.1.call-start = ((), (), s32[]{:S(2)}) async-start(), calls=%async_computation.6 | async-start | bytes 3145728 | tf_op jit(solution)/shard_map/all_gather | solution.py:113
  128.7 4.1 copy-start.1
  128.7 4.1 copy-start.3
  134.4 82.5 %reduce-scatter.7.cloned.1.call-start = ((), (), s32[]{:S(2)}) async-start(), calls=%async_computation.7 | async-start | bytes 3145728 | tf_op jit(solution)/shard_map/reduce_scatter | solution.py:116
  167.6 11.5 %copy-start.20 = (bf16[2048,1024]{1,0:T(8,128)(2,1)S(1)}, bf16[2048,1024]{1,0:T(8,128)(2,1)}, u32[]{:S(2)}) copy-start(bf16[2048,1024]{1,0:T(8,128)(2,1)} %param.20) | copy-start | bytes 12582916
  177.1 2.0 copy-start.27
  184.8 35.2 %copy-start.13 = (f32[1024]{0:T(1024)S(1)}, f32[1024]{0:T(1024)}, u32[]{:S(2)}) copy-start(f32[1024]{0:T(1024)} %param.23) | copy-start | bytes 12292
  184.8 72.9 %all-gather.9.cloned.1.call-start = ((), (), s32[]{:S(2)}) async-start(), calls=%async_computation.8 | async-start | bytes 3145728 | tf_op jit(solution)/shard_map/all_gather | solution.py:128
  216.8 3.2 copy-start.8
  219.6 2.0 copy-start.19
  224.5 83.4 %reduce-scatter.9.cloned.1.call-start = ((), (), s32[]{:S(2)}) async-start(), calls=%async_computation.9 | async-start | bytes 3145728 | tf_op jit(solution)/shard_map/reduce_scatter | solution.py:133
  257.7 12.3 %copy-start.21 = (bf16[1024,2048]{1,0:T(8,128)(2,1)S(1)}, bf16[1024,2048]{1,0:T(8,128)(2,1)}, u32[]{:S(2)}) copy-start(bf16[1024,2048]{1,0:T(8,128)(2,1)} %param.19) | copy-start | bytes 12582916
  268.0 2.0 copy-start.25
  275.8 72.3 %all-gather.11.cloned.1.call-start = ((), (), s32[]{:S(2)}) async-start(), calls=%async_computation.10 | async-start | bytes 3145728 | tf_op jit(solution)/shard_map/all_gather | solution.py:144
  307.8 4.4 copy-start.2
  307.8 4.4 copy-start.4
  307.8 4.4 copy-start.5
  307.8 4.4 copy-start.9
  314.9 155.7 %reduce-scatter.11.cloned.1.call-start = ((), (), s32[]{:S(2)}) async-start(), calls=%async_computation.11 | async-start | bytes 3145728 | tf_op jit(solution)/shard_map/reduce_scatter | solution.py:183
  361.3 1.6 copy-start.6
  381.1 1.6 copy-start.6
  405.9 270.6 %all-reduce.4.cloned.1.call-start = ((), (), s32[]{:S(2)}) async-start(), calls=%async_computation.12 | async-start | bytes 25165824 | tf_op jit(solution)/shard_map/psum | solution.py:193
  406.1 9.6 %copy-start.24 = (bf16[1024,1024]{1,0:T(8,128)(2,1)S(1)}, bf16[1024,1024]{1,0:T(8,128)(2,1)}, u32[]{:S(2)}) copy-start(bf16[1024,1024]{1,0:T(8,128)(2,1)} %all-gather.7.cloned.1.call-done) | copy-start | bytes 6291460
  406.1 9.6 %copy-start.26 = (bf16[1024,2048]{1,0:T(8,128)(2,1)S(1)}, bf16[1024,2048]{1,0:T(8,128)(2,1)}, u32[]{:S(2)}) copy-start(bf16[1024,2048]{1,0:T(8,128)(2,1)} %copy-done.25) | copy-start | bytes 12582916
  415.7 6.3 copy-start.10
  415.7 6.3 copy-start.11
  415.7 8.5 %copy-start.23 = (bf16[1024,1024]{1,0:T(8,128)(2,1)S(1)}, bf16[1024,1024]{1,0:T(8,128)(2,1)}, u32[]{:S(2)}) copy-start(bf16[1024,1024]{1,0:T(8,128)(2,1)} %all-gather.5.cloned.1.call-done) | copy-start | bytes 6291460
  422.0 2.3 copy-start.22
  429.1 0.7 copy-start.14
  429.1 0.7 copy-start.15
  429.1 0.7 copy-start.17
  429.1 0.7 copy-start.18
  676.4 6.8 copy-start.7
Sparse Core Ops, SparseCore 0:
  9.5 35.8 all-gather.4
  96.8 31.8 reduce-scatter.4
  134.5 33.0 all-gather.6
  184.9 31.8 reduce-scatter.6
  224.6 33.0 all-gather.8
  275.9 31.8 reduce-scatter.8
  315.0 33.0 all-gather.10
  406.0 31.9 reduce-scatter.10
  443.1 233.2 all-reduce.3
where the time goes:
time: 711 us; the launch traced here: 703 us
  waiting for transfers between devices  435 us (61%)
  matrix products  102 us (14%)
  local copies, waits for them, and re-layouts  59.5 us (8%)
  other arithmetic  49.6 us (7%)
  blocking collectives  40.7 us (6%)
  between operations  14.3 us (2%)
    psum x1, waiting for transfers between devices, body(): lax.psum(grad_qkv_w.astype(jnp.bfloat16), 'dp').astype(jnp.float32)  203 us
    psum x1, blocking collectives, body(): lax.psum((grad_gain1, grad_bias1, grad_gain2, grad_bias2), ('dp', 'tensor'))  40.7 us
    all_gather x1, waiting for transfers between devices, body(): source = lax.all_gather(layer_input, 'tensor', axis=0, tiled=True)  36.6 us
    all_gather x1, waiting for transfers between devices, body(): attn_group = lax.all_gather(attn_low, 'tensor', axis=0, tiled=True)  33.2 us
    all_gather x1, waiting for transfers between devices, body(): hidden_group = lax.all_gather(hidden_low, 'tensor', axis=0, tiled=True)  33 us
    all_gather x1, waiting for transfers between devices, body(): branch_group = lax.all_gather(branch_low, 'tensor', axis=0, tiled=True)  33 us
    reduce_scatter x1, waiting for transfers between devices, body(): lax.psum_scatter(jnp.dot(attended, out_use, preferred_element_type=jnp.fl...  32 us
    reduce_scatter x1, waiting for transfers between devices, body(): lax.psum_scatter(contract_cols(grad_upper, w_up).astype(jnp.bfloat16), 't...  32 us
  transfers between devices with their start and end apart: 9, of which 8 were waited for; matrix products, arithmetic and copies ran while one was open for 4% of the time, Pallas kernels for 0%

commit v1 on v0

--- a/solution.py
+++ b/solution.py
@@ -190,7 +190,7 @@
     ).astype(jnp.float32)
     grad_input = grad_first + input_part
     summed_qkv, summed_out, summed_up, summed_down = (
-        lax.psum(grad_qkv_w.astype(jnp.bfloat16), "dp").astype(jnp.float32),
+        jnp.sum(lax.all_gather(grad_qkv_w.astype(jnp.bfloat16), "dp"), axis=0).astype(jnp.float32),
         lax.psum(grad_out_w.astype(jnp.bfloat16), "dp").astype(jnp.float32),
         lax.psum(grad_up.astype(jnp.bfloat16), "dp").astype(jnp.float32),
         lax.psum(grad_down.astype(jnp.bfloat16), "dp").astype(jnp.float32),

time: 711 us -> 967 us (1.36)
  waiting for transfers between devices: 435 us -> 617 us
  local copies, waits for them, and re-layouts: 59.5 us -> 104 us
  other arithmetic: 49.6 us -> 75.4 us
    all_gather x0 -> x1, waiting for transfers between devices: none -> 233 us  [body(): lax.all_gather(grad_qkv_w.astype(jnp.bfloat16), 'dp')]
    psum x1, waiting for transfers between devices: 203 us -> 151 us  [body(): lax.psum(grad_out_w.astype(jnp.bfloat16), 'dp').astype(jnp.float32)]
    unnamed x55 -> x52, local copies, waits for them, and re-layouts: 10.2 us -> 54.8 us
    reduce_sum x0 -> x1, other arithmetic: none -> 24.6 us  [body(): jnp.sum(lax.all_gather(grad_qkv_w.astype(jnp.bfloat16), 'dp'), axis=0)]
  transfers between devices with their start and end apart: 9 -> 10, of which waited for: 8 -> 9; matrix products, arithmetic and copies ran while one was open for 4% -> 5% of each run, Pallas kernels for 0% -> 0%
where the time goes in v1:
time: 967 us; the launch traced here: 958 us
  waiting for transfers between devices  617 us (64%)
  matrix products  105 us (11%)
  local copies, waits for them, and re-layouts  104 us (11%)
  other arithmetic  75.4 us (8%)
  blocking collectives  41 us (4%)
  between operations  14.8 us (2%)
    all_gather x1, waiting for transfers between devices, body(): lax.all_gather(grad_qkv_w.astype(jnp.bfloat16), 'dp')  233 us
    psum x1, waiting for transfers between devices, body(): lax.psum(grad_out_w.astype(jnp.bfloat16), 'dp').astype(jnp.float32)  151 us
    unnamed x52, local copies, waits for them, and re-layouts  54.8 us
    psum x1, blocking collectives, body(): lax.psum((grad_gain1, grad_bias1, grad_gain2, grad_bias2), ('dp', 'tensor'))  41 us
    all_gather x1, waiting for transfers between devices, body(): source = lax.all_gather(layer_input, 'tensor', axis=0, tiled=True)  36.6 us
    all_gather x1, waiting for transfers between devices, body(): attn_group = lax.all_gather(attn_low, 'tensor', axis=0, tiled=True)  33.2 us
    all_gather x1, waiting for transfers between devices, body(): hidden_group = lax.all_gather(hidden_low, 'tensor', axis=0, tiled=True)  33 us
    all_gather x1, waiting for transfers between devices, body(): branch_group = lax.all_gather(branch_low, 'tensor', axis=0, tiled=True)  32.8 us
  transfers between devices with their start and end apart: 10, of which 9 were waited for; matrix products, arithmetic and copies ran while one was open for 5% of the time, Pallas kernels for 0%

profile of v1, /device:TPU:0, one launch (start us, length us, event | category | flops | bytes accessed | tf_op | source)
XLA Modules:
  0.0 958.3 jit_solution(9449035254353323641)
XLA Ops:
  8.8 36.6 %all-gather.7.cloned.1.call-done = bf16[1024,1024]{1,0:T(8,128)(2,1)} async-done(((bf16[512,1024]{1,0:T(8,128)(2,1)}), bf16[1024,1024]{1,0:T(8,128)(2,1)}) %all-gather.7.cloned.1.call-update) | async-done | bytes 2097168 | tf_op jit(solution)/shard_map/all_gather | solution.py:77
  45.4 6.3 convolution_convert_fusion.2
  51.7 8.9 reshape.243
  60.6 7.6 copy.46
  68.2 24.2 %while.22 = (s32[]{:T(128)}, bf16[2,512,512]{2,1,0:T(8,128)(2,1)}, f32[2,8,512]{2,1,0:T(8,128)S(1)}, bf16[2,512,3,8,64]{1,4,3,2,0:T(8,128)(2,1)}, s32[2,512]{1,0:T(2,128)S(1)}, /*index=5*/s32[]{:T(128)}) while((s32[]{:T(128)}, bf16[2,512,512]{2,1,0:T(8,128)(2,1)}, f32[2,8,512]{2,1,0:T(8,128)S(1)}, bf16[2,512,3,8,64]{1,4,3,2,0:T(8,128)(2,1)}, ...), condition=%wide.region_3.4_spmd, body=%wide.region_0.3_spmd.sunk | while | flops 562556928 | bytes 33691740 | solution.py:101
  73.2 3.2 fusion.87
  85.3 3.2 fusion.87
  92.5 4.1 convolution_convert_fusion.5
  96.7 32.0 %reduce-scatter.5.cloned.1.call-done = bf16[512,1024]{1,0:T(8,128)(2,1)} async-done(((bf16[1024,1024]{1,0:T(8,128)(2,1)}), bf16[512,1024]{1,0:T(8,128)(2,1)}) %reduce-scatter.5.cloned.1.call-update) | async-done | bytes 1048592 | tf_op jit(solution)/shard_map/reduce_scatter | solution.py:103
  134.6 33.0 %all-gather.9.cloned.1.call-done = bf16[1024,1024]{1,0:T(8,128)(2,1)} async-done(((bf16[512,1024]{1,0:T(8,128)(2,1)}), bf16[1024,1024]{1,0:T(8,128)(2,1)}) %all-gather.9.cloned.1.call-update) | async-done | bytes 2097168 | tf_op jit(solution)/shard_map/all_gather | solution.py:113
  167.6 9.5 multiply_convert_fusion.1
  179.1 5.7 convolution_convert_fusion.4
  184.8 32.0 %reduce-scatter.7.cloned.1.call-done = bf16[512,1024]{1,0:T(8,128)(2,1)} async-done(((bf16[1024,1024]{1,0:T(8,128)(2,1)}), bf16[512,1024]{1,0:T(8,128)(2,1)}) %reduce-scatter.7.cloned.1.call-update) | async-done | bytes 1048592 | tf_op jit(solution)/shard_map/reduce_scatter | solution.py:116
  216.8 2.8 fusion.49
  221.6 2.9 fusion.47
  224.9 32.8 %all-gather.11.cloned.1.call-done = bf16[1024,1024]{1,0:T(8,128)(2,1)} async-done(((bf16[512,1024]{1,0:T(8,128)(2,1)}), bf16[1024,1024]{1,0:T(8,128)(2,1)}) %all-gather.11.cloned.1.call-update) | async-done | bytes 2097168 | tf_op jit(solution)/shard_map/all_gather | solution.py:128
  257.7 10.3 %fusion.31 = bf16[1024,2048]{1,0:T(8,128)(2,1)S(1)} fusion(f32[1024,2048]{1,0:T(8,128)} %get-tuple-element.165, bf16[1024,1024]{1,0:T(8,128)(2,1)} %all-gather.11.cloned.1.call-done, bf16[2048,1024]{1,0:T(8,128)(2,1)} %param.20), kind=kOutput, calls=%fused_computation.54 | convolution fusion | flops 4315938816 | bytes 18874368 | tf_op jit(solution)/shard_map/dot_general | solution.py:55
  270.0 5.7 convolution_convert_fusion.3
  275.8 32.0 %reduce-scatter.9.cloned.1.call-done = bf16[512,1024]{1,0:T(8,128)(2,1)} async-done(((bf16[1024,1024]{1,0:T(8,128)(2,1)}), bf16[512,1024]{1,0:T(8,128)(2,1)}) %reduce-scatter.9.cloned.1.call-update) | async-done | bytes 1048592 | tf_op jit(solution)/shard_map/reduce_scatter | solution.py:133
  307.8 4.4 multiply_reduce_fusion.1
  312.3 2.5 fusion.46
  314.9 33.2 %all-gather.13.cloned.1.call-done = bf16[1024,1024]{1,0:T(8,128)(2,1)} async-done(((bf16[512,1024]{1,0:T(8,128)(2,1)}), bf16[1024,1024]{1,0:T(8,128)(2,1)}) %all-gather.13.cloned.1.call-update) | async-done | bytes 2097168 | tf_op jit(solution)/shard_map/all_gather | solution.py:144
  348.1 4.1 convolution_convert_fusion.7
  352.2 4.0 reshape.242
  356.3 3.3 copy.50
  359.6 39.5 %while.23 = (s32[]{:T(128)}, bf16[2,512,3,512]{3,1,0,2:T(8,128)(2,1)}, bf16[2,512,3,8,64]{1,4,3,2,0:T(8,128)(2,1)}, s32[2,512]{1,0:T(2,128)S(1)}, f32[2,8,512]{2...) while((s32[]{:T(128)}, bf16[2,512,3,512]{3,1,0,2:T(8,128)(2,1)}, ...), condition=%wide.region_17.18_spmd, body=%wide.region_15.17_spmd.sunk | while | flops 1376776192 | bytes 86104192 | solution.py:178
  364.9 2.9 multiply_reduce_fusion.7
  367.9 2.7 multiply_convert_fusion.3
  374.0 2.6 copy.73
  376.6 2.7 constant_dynamic-update-slice_fusion.5
  384.7 2.9 multiply_reduce_fusion.7
  387.6 2.7 multiply_convert_fusion.3
  393.8 2.6 copy.73
  396.4 2.6 constant_dynamic-update-slice_fusion.5
  399.0 6.6 bitcast_convert_fusion
  405.9 9.6 %convolution_convert_fusion = bf16[2048,1024]{1,0:T(8,128)(2,1)} fusion(bf16[1024,2048]{1,0:T(8,128)(2,1)} %copy-done.25, bf16[1024,1024]{1,0:T(8,128)(2,1)} %all-gather.11.cloned.1.call-done), kind=kOutput, calls=%fused_computation.58 | convolution fusion | flops 4297064448 | bytes 10485760 | tf_op jit(solution)/shard_map/dot_general | solution.py:49
  415.5 6.2 convolution_convert_fusion.1
  424.0 7.7 convert_bitcast_fusion
  432.5 41.0 %all-reduce = (f32[1024]{0:T(1024)}, f32[1024]{0:T(1024)}, f32[1024]{0:T(1024)}, f32[1024]{0:T(1024)}) all-reduce(f32[1024]{0:T(1024)S(1)} %copy-done.17, f32[1024]{0:T(1024)S(1)} %copy-done.18, f32[1024]{0:T(1024)S(1)} %copy-done.14, f32[1024]{0:T(1024)S(1)} %copy-done.15), channel_id=1, replica_groups=mesh['dp'=16,'tensor'=2] {'dp','tensor'}, use_global_device_ids=true, to_apply=%region_24.25 | all-reduce | flops 4096 | bytes 32768 | tf_op jit(solution)/shard_map/psum | solution.py:198
  473.5 3.2 add_convert_fusion
  476.7 151.2 %all-reduce.4.cloned.1.call-done = (bf16[512,1024]{1,0:T(8,128)(2,1)}, bf16[1024,2048]{1,0:T(8,128)(2,1)}, bf16[2048,1024]{1,0:T(8,128)(2,1)}) async-done(((bf16[512,1024]{1,0:T(8,128)(2,1)}, bf16[1024,2048]{1,0:T(8,128)(2,1)}, bf16[2048,1024]{1,0:T(8,128)(2,1)}), (bf16[512,1024]{1,0:T(8,128)(2,1)}, bf16[1024,2048]{1,0:T(8,128)(2,1)}, bf16[2048,1024]{1,0:T(8,128)(2,1)})) %all-reduce.4.cloned.1.call-update) | async-done | bytes 9437200 | tf_op jit(solution)/shard_map/psum | solution.py:194
  627.9 2.8 convert_element_type.142
  630.7 8.0 convert_element_type.144
  638.7 4.4 convert_element_type.146
  643.1 233.3 %all-gather.15.cloned.1.call-done = bf16[16384,3,512]{0,2,1:T(8,128)(2,1)} async-done(((bf16[1024,3,512]{0,2,1:T(8,128)(2,1)}), bf16[16384,3,512]{0,2,1:T(8,128)(2,1)}) %all-gather.15.cloned.1.call-update) | async-done | bytes 50331664 | tf_op jit(solution)/shard_map/all_gather | solution.py:193
  876.5 44.6 %copy.68 = bf16[192,8,16,1024]{3,2,1,0:T(8,128)(2,1)} copy(bf16[192,8,16,1024]{3,1,2,0:T(8,128)(2,1)} %bitcast.145) | data formatting | bytes 100663296
  921.1 24.6 %reduce_sum.146 = bf16[1024,3,512]{0,2,1:T(8,128)(2,1)} reduce(bf16[16,1024,3,512]{1,0,3,2:T(8,128)(2,1)} %bitcast.142, bf16[]{:T(256)} %constant.63.clone.1), dimensions={0}, to_apply=%region_19.20 | reduce | flops 23592960 | bytes 53477376 | tf_op jit(solution)/shard_map/reduce_sum | solution.py:193
  945.6 5.4 copy.53
  (126 shorter events, 52.9 us)
Async XLA Ops:
  7.2 38.2 %copy-start = (bf16[1024,3,512]{2,0,1:T(8,128)(2,1)S(1)}, bf16[1024,3,512]{2,0,1:T(8,128)(2,1)}, u32[]{:S(2)}) copy-start(bf16[1024,3,512]{2,0,1:T(8,128)(2,1)} %param.17) | copy-start | bytes 9437188
  7.2 38.2 %all-gather.7.cloned.1.call-start = ((), (), s32[]{:S(2)}) async-start(), calls=%async_computation.4 | async-start | bytes 3145728 | tf_op jit(solution)/shard_map/all_gather | solution.py:77
  7.9 120.8 %reduce-scatter.5.cloned.1.call-start = ((), (), s32[]{:S(2)}) async-start(), calls=%async_computation.5 | async-start | bytes 3145728 | tf_op jit(solution)/shard_map/reduce_scatter | solution.py:103
  96.6 36.2 %copy-start.12 = (f32[1024]{0:T(1024)S(1)}, f32[1024]{0:T(1024)}, u32[]{:S(2)}) copy-start(f32[1024]{0:T(1024)} %param.21) | copy-start | bytes 12292
  96.6 36.2 %copy-start.16 = (f32[1024]{0:T(1024)S(1)}, f32[1024]{0:T(1024)}, u32[]{:S(2)}) copy-start(f32[1024]{0:T(1024)} %param.22) | copy-start | bytes 12292
  96.6 71.0 %all-gather.9.cloned.1.call-start = ((), (), s32[]{:S(2)}) async-start(), calls=%async_computation.6 | async-start | bytes 3145728 | tf_op jit(solution)/shard_map/all_gather | solution.py:113
  128.7 4.1 copy-start.1
  128.7 4.1 copy-start.3
  134.3 82.5 %reduce-scatter.7.cloned.1.call-start = ((), (), s32[]{:S(2)}) async-start(), calls=%async_computation.7 | async-start | bytes 3145728 | tf_op jit(solution)/shard_map/reduce_scatter | solution.py:116
  167.6 11.5 %copy-start.20 = (bf16[2048,1024]{1,0:T(8,128)(2,1)S(1)}, bf16[2048,1024]{1,0:T(8,128)(2,1)}, u32[]{:S(2)}) copy-start(bf16[2048,1024]{1,0:T(8,128)(2,1)} %param.20) | copy-start | bytes 12582916
  177.1 2.0 copy-start.25
  184.7 35.2 %copy-start.13 = (f32[1024]{0:T(1024)S(1)}, f32[1024]{0:T(1024)}, u32[]{:S(2)}) copy-start(f32[1024]{0:T(1024)} %param.23) | copy-start | bytes 12292
  184.8 72.9 %all-gather.11.cloned.1.call-start = ((), (), s32[]{:S(2)}) async-start(), calls=%async_computation.8 | async-start | bytes 3145728 | tf_op jit(solution)/shard_map/all_gather | solution.py:128
  216.8 3.2 copy-start.8
  219.6 2.0 copy-start.19
  224.4 83.4 %reduce-scatter.9.cloned.1.call-start = ((), (), s32[]{:S(2)}) async-start(), calls=%async_computation.9 | async-start | bytes 3145728 | tf_op jit(solution)/shard_map/reduce_scatter | solution.py:133
  257.7 12.3 %copy-start.21 = (bf16[1024,2048]{1,0:T(8,128)(2,1)S(1)}, bf16[1024,2048]{1,0:T(8,128)(2,1)}, u32[]{:S(2)}) copy-start(bf16[1024,2048]{1,0:T(8,128)(2,1)} %param.19) | copy-start | bytes 12582916
  268.0 2.0 copy-start.23
  275.7 72.4 %all-gather.13.cloned.1.call-start = ((), (), s32[]{:S(2)}) async-start(), calls=%async_computation.10 | async-start | bytes 3145728 | tf_op jit(solution)/shard_map/all_gather | solution.py:144
  307.8 4.4 copy-start.2
  307.8 4.4 copy-start.4
  307.8 4.4 copy-start.5
  307.8 4.4 copy-start.9
  314.8 158.7 %reduce-scatter.11.cloned.1.call-start = ((), (), s32[]{:S(2)}) async-start(), calls=%async_computation.11 | async-start | bytes 3145728 | tf_op jit(solution)/shard_map/reduce_scatter | solution.py:183
  361.3 1.3 copy-start.6
  381.1 1.3 copy-start.6
  405.6 222.3 %all-reduce.4.cloned.1.call-start = ((), (), s32[]{:S(2)}) async-start(), calls=%async_computation.13 | async-start | bytes 18874368 | tf_op jit(solution)/shard_map/psum | solution.py:194
  405.9 9.6 %copy-start.22 = (bf16[1024,1024]{1,0:T(8,128)(2,1)S(1)}, bf16[1024,1024]{1,0:T(8,128)(2,1)}, u32[]{:S(2)}) copy-start(bf16[1024,1024]{1,0:T(8,128)(2,1)} %all-gather.9.cloned.1.call-done) | copy-start | bytes 6291460
  405.9 9.6 %copy-start.24 = (bf16[1024,2048]{1,0:T(8,128)(2,1)S(1)}, bf16[1024,2048]{1,0:T(8,128)(2,1)}, u32[]{:S(2)}) copy-start(bf16[1024,2048]{1,0:T(8,128)(2,1)} %copy-done.23) | copy-start | bytes 12582916
  415.5 6.3 copy-start.10
  415.5 6.3 copy-start.11
  424.0 452.5 %all-gather.15.cloned.1.call-start = ((), (), s32[]{:S(2)}) async-start(), calls=%async_computation.12 | async-start | bytes 53477376 | tf_op jit(solution)/shard_map/all_gather | solution.py:193
  431.7 0.7 copy-start.14
  431.7 0.7 copy-start.15
  431.7 0.7 copy-start.17
  431.7 0.7 copy-start.18
  630.7 8.0 copy-start.7
Sparse Core Ops, SparseCore 0:
  9.5 35.8 all-gather.6
  96.7 31.8 reduce-scatter.4
  134.5 33.0 all-gather.8
  184.9 31.8 reduce-scatter.6
  224.6 33.0 all-gather.10
  275.8 31.9 reduce-scatter.8
  315.0 33.0 all-gather.12
  405.7 31.8 reduce-scatter.10
  442.2 185.5 all-reduce.3
  629.3 247.1 all-gather.14
